TPU v7x, 32 devices: a whole 2x2x4 slice. The times are simulated.
32 devices in a mesh: grp: 4 (over y, x), mem: 8 (over z, core).
Axes of the slice: x: 2, y: 2, z: 4, core: 2. Of those that a mesh axis runs over, the one named last changes fastest.
Arguments:
- values: bfloat16 [32, 8, 32, 128], P(('grp', 'mem')), may hold values from -6 to 6
- slots: int32 [32, 8, 32], P(('grp', 'mem')), may hold values from 0 to 7167
- counts: int32 [32, 8], P(('grp', 'mem')), may hold values from 0 to 32, as said below
Outputs:
- averaged: float32 [57344, 128], P('mem')
- returned: bfloat16 [32, 8, 32, 128], P(('grp', 'mem'))
Inputs may be any that keep to these rules, and one draw needn't show every extreme that they name: `counts`: every device has at least one list with exactly 32 valid entries.
All inputs are finite; a program needn't handle non-finite values.
Results may differ from a plain program's by a relative error of at most 0.0024.
Values may be sent and summed in bfloat16 or wider, within the bound.
A program may use at most 64 MiB of HBM per device.

v0:
```python
import math

import jax
import jax.numpy as jnp
from jax import lax
from jax.sharding import PartitionSpec as P

BUCKET = 7168


def tiled_sums(rows_in, slot_in):
    lane_count = rows_in.shape[1]
    tile = math.gcd(BUCKET, 1024)

    def one_tile(first):
        wanted = first + lax.broadcasted_iota(jnp.int32, (tile, 1), 0)
        onehot = (wanted == slot_in[None, :]).astype(jnp.bfloat16)
        return jnp.dot(onehot, rows_in, preferred_element_type=jnp.float32)

    starts = jnp.arange(BUCKET // tile, dtype=jnp.int32) * tile
    return lax.map(one_tile, starts).reshape(BUCKET, lane_count)


def live_counts(slot_in):
    live_in = (slot_in >= 0).astype(jnp.float32)
    return jax.ops.segment_sum(live_in, jnp.maximum(slot_in, 0), num_segments=BUCKET)


def per_device(values, slots, counts):
    blocks_out = values[0]
    slot_ids = slots[0]
    list_counts = counts[0]
    members, capacity, lane_count = blocks_out.shape
    is_valid = lax.broadcasted_iota(jnp.int32, (members, capacity), 1) < list_counts[:, None]
    send_blocks = jnp.where(is_valid[:, :, None], blocks_out, jnp.zeros_like(blocks_out))
    send_slots = jnp.where(is_valid, slot_ids, -1)
    got_blocks, got_slots = (
        lax.all_to_all(send_blocks, "mem", split_axis=0, concat_axis=0, tiled=True),
        lax.all_to_all(send_slots, "mem", split_axis=0, concat_axis=0, tiled=True),
    )
    rows_in = got_blocks.reshape(members * capacity, lane_count)
    slot_in = got_slots.reshape(members * capacity)
    slot_count = None
    local_sums = tiled_sums(rows_in, slot_in)
    payload = (local_sums, live_counts(slot_in))
    reduced = lax.psum(payload, "grp")
    total_count = reduced[1]
    averaged = reduced[0] / jnp.maximum(total_count, 1.0)[:, None]
    owned_rows = jnp.take(averaged, jnp.maximum(slot_in, 0), axis=0)
    back_rows = jnp.where((slot_in >= 0)[:, None], owned_rows, 0.0).astype(jnp.bfloat16)
    back_rows = back_rows.reshape(members, capacity, lane_count)
    returned = lax.all_to_all(back_rows, "mem", split_axis=0, concat_axis=0, tiled=True)
    return (averaged, returned[None])


def solution(mesh):
    return jax.shard_map(
        per_device,
        mesh=mesh,
        in_specs=(
            P(("grp", "mem"), None, None, None),
            P(("grp", "mem"), None, None),
            P(("grp", "mem"), None),
        ),
        out_specs=(P("mem", None), P(("grp", "mem"), None, None, None)),
        check_vma=False,
    )
```

profile of v0, /device:TPU:0, one launch (start us, length us, event | category | flops | bytes accessed | tf_op | source)
XLA Modules:
  0.0 168.0 jit_solution(9887654835759522025)
XLA Ops:
  7.2 1.4 compare_select_fusion
  8.5 6.4 %all-to-all-start = ((s32[8,1,32]{2,1,0:T(1,128)}), s32[8,1,32]{2,1,0:T(1,128)S(1)}, u32[]{:S(2)}, u32[]{:S(2)}) async-start(s32[8,1,32]{2,1,0:T(1,128)} %compare_select_fusion), calls=%async_computation | async-start | bytes 8192 | tf_op jit(solution)/shard_map/all_to_all | solution.py:39
  14.9 0.7 iota_compare_fusion
  15.6 1.6 bitcast_select_fusion
  17.2 3.2 %all-to-all-done = s32[8,1,32]{2,1,0:T(1,128)S(1)} async-done(((s32[8,1,32]{2,1,0:T(1,128)}), s32[8,1,32]{2,1,0:T(1,128)S(1)}, u32[]{:S(2)}, u32[]{:S(2)}) %all-to-all-start) | async-done | bytes 1056 | tf_op jit(solution)/shard_map/all_to_all | solution.py:39
  20.4 3.4 %all-to-all-start.1 = ((bf16[8,32,128]{2,1,0:T(8,128)(2,1)}), bf16[8,32,128]{2,1,0:T(8,128)(2,1)S(1)}, u32[]{:S(2)}, u32[]{:S(2)}) async-start(bf16[8,32,128]{2,1,0:T(8,128)(2,1)} %bitcast_select_fusion), calls=%async_computation.1 | async-start | bytes 131072 | tf_op jit(solution)/shard_map/all_to_all | solution.py:38
  23.9 5.7 %all-to-all-done.1 = bf16[8,32,128]{2,1,0:T(8,128)(2,1)S(1)} async-done(((bf16[8,32,128]{2,1,0:T(8,128)(2,1)}), bf16[8,32,128]{2,1,0:T(8,128)(2,1)S(1)}, u32[]{:S(2)}, u32[]{:S(2)}) %all-to-all-start.1) | async-done | bytes 65568 | tf_op jit(solution)/shard_map/all_to_all | solution.py:38
  29.6 16.7 %while.11 = (s32[]{:T(128)}, f32[7,1024,128]{2,1,0:T(8,128)}, s32[7]{0:T(128)S(1)}, s32[8,32]{1,0:T(8,128)}, bf16[256,128]{1,0:T(8,128)(2,1)S(1)}, /*index=5*/s32[256]{0:T(256)S(1)}, s32[]{:T(128)}) while((s32[]{:T(128)}, f32[7,1024,128]{2,1,0:T(8,128)}, s32[7]{0:T(128)S(1)}, s32[8,32]{1,0:T(8,128)}, bf16[256,128]{1,0:T(8,128)(2,1)S(1)}, ...), condition=%wide.wide.region_1.2_spmd, body=%wide.wide.region_0.1_spmd.sunk | while | flops 67372032 | bytes 599645 | solution.py:21
  30.2 0.6 iota_add_fusion.3
  30.8 1.2 fusion.16
  32.6 0.6 iota_add_fusion.3
  33.2 1.2 fusion.16
  35.6 1.2 fusion.16
  37.4 0.6 iota_add_fusion.3
  38.0 1.2 fusion.16
  40.4 1.2 fusion.16
  42.8 1.2 fusion.16
  45.2 1.2 fusion.16
  47.2 2.0 %scatter_custom_fusion = f32[7168]{0:T(1024)S(1)} fusion(s32[256]{0:T(256)S(1)} %reshape.145, f32[256]{0:T(256)S(1)} %reshape.147, f32[]{:T(128)} %constant.16.clone.1), kind=kCustom, calls=%fused_computation.14 | custom fusion | flops 256 | bytes 28676 | tf_op jit(solution)/shard_map/scatter-add | solution.py:26
  49.2 17.7 %psum.15 = f32[7168]{0:T(1024)S(1)} all-reduce(f32[7168]{0:T(1024)S(1)} %scatter_custom_fusion), channel_id=1, replica_groups=mesh['grp'=4,'mem'=8] {'grp'}, use_global_device_ids=true, to_apply=%region_4.5 | all-reduce | flops 7168 | bytes 57344 | tf_op jit(solution)/shard_map/psum | solution.py:46
  67.0 74.6 %all-reduce.2.cloned.1.call-done = f32[7168,128]{1,0:T(8,128)} async-done(((f32[7168,128]{1,0:T(8,128)}), f32[7168,128]{1,0:T(8,128)}) %all-reduce.2.cloned.1.call-update) | async-done | bytes 3670032 | tf_op jit(solution)/shard_map/psum | solution.py:46
  141.6 5.7 %broadcast_divide_fusion = f32[7168,128]{1,0:T(8,128)} fusion(f32[7168,128]{1,0:T(8,128)} %all-reduce.2.cloned.1.call-done, f32[7168]{0:T(1024)S(1)} %broadcast_maximum_fusion), kind=kLoop, calls=%fused_computation.8 | loop fusion | flops 917504 | bytes 7368704 | tf_op jit(solution)/shard_map/div | solution.py:48
  147.3 2.8 %gather_fusion = bf16[256,128]{1,0:T(8,128)(2,1)S(1)} fusion(f32[7168,128]{1,0:T(8,128)} %broadcast_divide_fusion, s32[1024]{0:T(1024)S(1)} %pad_clamp_fusion), kind=kCustom, calls=%fused_computation | custom fusion | bytes 132096 | tf_op jit(solution)/shard_map/jit(_take)/gather | solution.py:49
  150.2 10.3 %all_to_all.19 = bf16[8,32,128]{2,1,0:T(8,128)(2,1)S(1)} all-to-all(bf16[8,32,128]{2,1,0:T(8,128)(2,1)S(1)} %select_convert_fusion), channel_id=1, replica_groups=mesh['grp'=4,'mem'=8] {'mem'}, dimensions={0} | all-to-all | bytes 131072 | tf_op jit(solution)/shard_map/all_to_all | solution.py:52
  (29 shorter events, 8.4 us)
Async XLA Ops:
  8.5 11.9 %all-to-all-start = ((s32[8,1,32]{2,1,0:T(1,128)}), s32[8,1,32]{2,1,0:T(1,128)S(1)}, u32[]{:S(2)}, u32[]{:S(2)}) async-start(s32[8,1,32]{2,1,0:T(1,128)} %compare_select_fusion), calls=%async_computation | async-start | bytes 8192 | tf_op jit(solution)/shard_map/all_to_all | solution.py:39
  20.4 9.2 %copy-start = (s32[8,1,32]{2,1,0:T(1,128)}, s32[8,1,32]{2,1,0:T(1,128)S(1)}, u32[]{:S(2)}) copy-start(s32[8,1,32]{2,1,0:T(1,128)S(1)} %all-to-all-done) | copy-start | bytes 3076
  20.4 9.2 %all-to-all-start.1 = ((bf16[8,32,128]{2,1,0:T(8,128)(2,1)}), bf16[8,32,128]{2,1,0:T(8,128)(2,1)S(1)}, u32[]{:S(2)}, u32[]{:S(2)}) async-start(bf16[8,32,128]{2,1,0:T(8,128)(2,1)} %bitcast_select_fusion), calls=%async_computation.1 | async-start | bytes 131072 | tf_op jit(solution)/shard_map/all_to_all | solution.py:38
  23.8 117.8 %all-reduce.2.cloned.1.call-start = ((), (), s32[]{:S(2)}) async-start(), calls=%async_computation.3 | async-start | bytes 7340032 | tf_op jit(solution)/shard_map/psum | solution.py:46
  46.3 0.7 copy-start.1
Sparse Core Ops, SparseCore 0:
  46.5 95.0 all-reduce.1
where the time goes:
time: 169 us; the launch traced here: 168 us
  waiting for transfers between devices  83.5 us (49%)
  blocking collectives  28 us (17%)
  other arithmetic  16.1 us (10%)
  between operations  14.1 us (8%)
  starting transfers between devices  9.75 us (6%)
  local copies, waits for them, and re-layouts  8.36 us (5%)
  matrix products  8.07 us (5%)
    psum x1, waiting for transfers between devices, per_device(): reduced = lax.psum(payload, 'grp')  74.6 us
    psum x1, blocking collectives, per_device(): reduced = lax.psum(payload, 'grp')  17.7 us
    all_to_all x1, blocking collectives, per_device(): lax.all_to_all(back_rows, 'mem', split_axis=0, concat_axis=0, tiled=True)  10.3 us
    dot_general x7, matrix products, one_tile(): return jnp.dot(onehot, rows_in, preferred_element_type=jnp.float32)  8.07 us
    all_to_all x1, starting transfers between devices, per_device(): lax.all_to_all(send_slots, 'mem', split_axis=0, concat_axis=0, tiled=True)  6.35 us
    div x1, other arithmetic, per_device(): averaged = reduced[0] / jnp.maximum(total_count, 1.0)[:, None]  5.72 us
    all_to_all x1, waiting for transfers between devices, per_device(): lax.all_to_all(send_blocks, 'mem', split_axis=0, concat_axis=0, tiled=True)  5.7 us
    add x7, other arithmetic, one_tile(): wanted = first + lax.broadcasted_iota(jnp.int32, (tile, 1), 0)  4.53 us
  transfers between devices with their start and end apart: 3, of which 3 were waited for; matrix products, arithmetic and copies ran while one was open for 3% of the time, Pallas kernels for 0%

commit v1 on v0

v1 whole, which is shorter than its diff:
```python
import functools

import jax
import jax.numpy as jnp
from jax import lax
from jax.experimental import pallas as pl
from jax.experimental.pallas import tpu as pltpu
from jax.sharding import PartitionSpec as P

BUCKET = 7168
LANES = 128
ROWS = 256
WIDE = 1024


def exchange_kernel(
    groups, members, cap,
    values_ref, slots_ref, counts_ref,
    avg_ref, lane_ref, back_ref,
    got, got_slots, own_slots, lane_f, ret,
    v_send, v_recv, s_send, s_recv,
    fv_send, fv_recv, fs_send, fs_recv,
    r_send, r_recv, local_sem,
):
    g = lax.axis_index("grp")
    m = lax.axis_index("mem")
    total = groups * members * cap
    per_row = LANES // cap

    barrier = pltpu.get_barrier_semaphore()
    for step in range(1, members):
        pl.semaphore_signal(barrier, inc=1, device_id={"mem": lax.rem(m + step, members)})
    for step in range(1, groups):
        pl.semaphore_signal(barrier, inc=1, device_id={"grp": lax.rem(g + step, groups)})

    raw = slots_ref[0]
    shown = jnp.concatenate([raw] * per_row, axis=1)
    row_id = lax.broadcasted_iota(jnp.int32, (members, LANES), 0)
    entry = lax.rem(lax.broadcasted_iota(jnp.int32, (members, LANES), 1), cap)
    limit = jnp.zeros((members, LANES), jnp.int32)
    for k in range(members):
        limit = jnp.where(row_id == k, counts_ref[0, k], limit)
    masked = jnp.where(entry < limit, shown, -1)
    for k in range(members):
        own_slots[k] = masked[k : k + 1, :]

    pl.semaphore_wait(barrier, members - 1 + groups - 1)

    mine = g * members + m

    def to_member(step):
        peer = lax.rem(m + step, members)
        return (
            pltpu.make_async_remote_copy(
                values_ref.at[0, peer], got.at[mine], v_send.at[step], v_recv.at[step],
                device_id={"mem": peer},
            ),
            pltpu.make_async_remote_copy(
                own_slots.at[peer], got_slots.at[mine], s_send.at[step], s_recv.at[step],
                device_id={"mem": peer},
            ),
        )

    def from_member(step):
        src = lax.rem(m + members - step, members)
        at = g * members + src
        return (
            pltpu.make_async_remote_copy(
                values_ref.at[0, src], got.at[at], v_send.at[step], v_recv.at[step],
                device_id={"mem": src},
            ),
            pltpu.make_async_remote_copy(
                own_slots.at[src], got_slots.at[at], s_send.at[step], s_recv.at[step],
                device_id={"mem": src},
            ),
        )

    def to_group(step, hop):
        src = lax.rem(m + members - step, members)
        at = g * members + src
        peer = lax.rem(g + hop, groups)
        return (
            pltpu.make_async_remote_copy(
                got.at[at], got.at[at], fv_send.at[step, hop], fv_recv.at[step, hop],
                device_id={"grp": peer},
            ),
            pltpu.make_async_remote_copy(
                got_slots.at[at], got_slots.at[at], fs_send.at[step, hop], fs_recv.at[step, hop],
                device_id={"grp": peer},
            ),
        )

    def from_group(step, hop):
        src = lax.rem(m + members - step, members)
        peer = lax.rem(g + groups - hop, groups)
        at = peer * members + src
        return (
            pltpu.make_async_remote_copy(
                got.at[at], got.at[at], fv_send.at[step, hop], fv_recv.at[step, hop],
                device_id={"grp": peer},
            ),
            pltpu.make_async_remote_copy(
                got_slots.at[at], got_slots.at[at], fs_send.at[step, hop], fs_recv.at[step, hop],
                device_id={"grp": peer},
            ),
        )

    local_v = pltpu.make_async_copy(values_ref.at[0, m], got.at[mine], local_sem.at[0])
    local_s = pltpu.make_async_copy(own_slots.at[m], got_slots.at[mine], local_sem.at[1])
    local_v.start()
    local_s.start()

    def each(low, high, body):
        if high - low <= 8:
            for k in range(low, high):
                body(k)
        else:
            lax.fori_loop(low, high, lambda k, c: (body(k), c)[1], 0)

    def start_members(step):
        for copy in to_member(step):
            copy.start()

    each(1, members, start_members)

    local_v.wait()
    local_s.wait()

    def forward(step):
        for hop in range(1, groups):
            for copy in to_group(step, hop):
                copy.start()

    forward(0)

    def pass_on(step):
        for copy in from_member(step):
            copy.wait_recv()
        forward(step)

    each(1, members, pass_on)

    def land(step):
        for hop in range(1, groups):
            for copy in from_group(step, hop):
                copy.wait_recv()

    each(0, members, land)

    lane = lax.broadcasted_iota(jnp.int32, (1, LANES), 1)

    def pack(k):
        row = got_slots[k * per_row]
        for q in range(1, per_row):
            row = jnp.where(lane >= q * cap, got_slots[k * per_row + q], row)
        lane_ref[pl.ds(k, 1), :] = row
        lane_f[pl.ds(k, 1), :] = row.astype(jnp.float32)

    each(0, total // LANES, pack)

    wide = min(WIDE, total)
    senders_wide = wide // cap
    halves = ROWS // LANES

    def block(b):
        columns = []
        for h in range(halves):
            row = lane_f[pl.ds(b * halves + h, 1), :]
            row = jnp.where(row < 0, -2.0, row)
            columns.append(jnp.transpose(jnp.broadcast_to(row, (LANES, LANES))))
        column = jnp.concatenate(columns, axis=0)

        def part(w):
            same = []
            for l in range(wide // LANES):
                row = lane_f[pl.ds(w * (wide // LANES) + l, 1), :]
                same.append(jnp.where(column == row, 1.0, 0.0).astype(jnp.bfloat16))
            onehot = jnp.concatenate(same, axis=1)
            rows = got[pl.ds(w * senders_wide, senders_wide)].reshape(wide, LANES)
            rows = jnp.concatenate([rows, jnp.ones((wide, LANES), jnp.bfloat16)], axis=1)
            return jnp.dot(onehot, rows, preferred_element_type=jnp.float32)

        if total == wide:
            acc = part(0)
        else:
            acc = lax.fori_loop(
                0, total // wide, lambda w, a: a + part(w), jnp.zeros((ROWS, 2 * LANES), jnp.float32)
            )
        avg = acc[:, :LANES] / jnp.maximum(acc[:, LANES:], 1.0)
        avg_ref[pl.ds(b * ROWS, ROWS), :] = avg
        return avg

    blocks_each = members * cap // ROWS
    senders_each = ROWS // cap

    def own_block(t):
        avg = block(g * blocks_each + t)
        ret[pl.ds(t * senders_each, senders_each)] = avg.astype(jnp.bfloat16).reshape(
            senders_each, cap, LANES
        )

    each(0, blocks_each, own_block)

    def back_to(step):
        peer = lax.rem(m + step, members)
        return pltpu.make_async_remote_copy(
            ret.at[peer], back_ref.at[m], r_send.at[step], r_recv.at[step],
            device_id={"mem": peer},
        )

    def back_from(step):
        src = lax.rem(m + members - step, members)
        return pltpu.make_async_remote_copy(
            ret.at[src], back_ref.at[src], r_send.at[step], r_recv.at[step],
            device_id={"mem": src},
        )

    each(1, members, lambda step: back_to(step).start())
    local_r = pltpu.make_async_copy(ret.at[m], back_ref.at[m], local_sem.at[2])
    local_r.start()

    for q in range(1, groups):
        other = lax.rem(g + q, groups)
        each(0, blocks_each, lambda t, other=other: (block(other * blocks_each + t), None)[1])

    def finish(step):
        for copy in to_member(step):
            copy.wait_send()
        back_to(step).wait_send()
        back_from(step).wait_recv()

    def finish_forward(step):
        for hop in range(1, groups):
            for copy in to_group(step, hop):
                copy.wait_send()

    each(0, members, finish_forward)
    local_r.wait()
    each(1, members, finish)


def place_kernel(total, avg_ref, slot_ref, back_ref, out_ref, returned_ref, table, sems):
    unroll = 16
    table[...] = jnp.zeros_like(table)
    returned_ref[...] = back_ref[...]

    def step(i, carry):
        base = pl.multiple_of(i * unroll, unroll)
        row = base // LANES
        col = lax.rem(base, LANES)
        for k in range(unroll):
            s = slot_ref[row, col + k]
            s = jnp.where(s < 0, BUCKET, s)
            table[pl.ds(s, 1), :] = avg_ref[pl.ds(base + k, 1), :]
        return carry

    lax.fori_loop(0, total // unroll, step, 0)
    pieces = sems.shape[0]
    size = BUCKET // pieces
    copies = [
        pltpu.make_async_copy(
            table.at[pl.ds(k * size, size)], out_ref.at[pl.ds(k * size, size)], sems.at[k]
        )
        for k in range(pieces)
    ]
    for copy in copies:
        copy.start()
    for copy in copies:
        copy.wait()


def per_device(groups, members, values, slots, counts):
    cap, lanes = values.shape[2:]
    total = groups * members * cap
    vmem = pl.BlockSpec(memory_space=pltpu.VMEM)
    smem = pl.BlockSpec(memory_space=pltpu.SMEM)
    dma = pltpu.SemaphoreType.DMA
    avg, lane_slots, back = pl.pallas_call(
        functools.partial(exchange_kernel, groups, members, cap),
        out_shape=(
            jax.ShapeDtypeStruct((total, lanes), jnp.float32),
            jax.ShapeDtypeStruct((total // LANES, LANES), jnp.int32),
            jax.ShapeDtypeStruct((members, cap, lanes), jnp.bfloat16),
        ),
        in_specs=[vmem, vmem, smem],
        out_specs=(vmem, vmem, vmem),
        scratch_shapes=[
            pltpu.VMEM((groups * members, cap, lanes), jnp.bfloat16),
            pltpu.VMEM((groups * members, 1, LANES), jnp.int32),
            pltpu.VMEM((members, 1, LANES), jnp.int32),
            pltpu.VMEM((total // LANES, LANES), jnp.float32),
            pltpu.VMEM((members, cap, lanes), jnp.bfloat16),
            dma((members,)), dma((members,)), dma((members,)), dma((members,)),
            dma((members, groups)), dma((members, groups)),
            dma((members, groups)), dma((members, groups)),
            dma((members,)), dma((members,)), dma((3,)),
        ],
        compiler_params=pltpu.CompilerParams(collective_id=0, has_side_effects=True),
    )(values, slots, counts)
    averaged, returned = pl.pallas_call(
        functools.partial(place_kernel, total),
        out_shape=(
            jax.ShapeDtypeStruct((BUCKET, lanes), jnp.float32),
            jax.ShapeDtypeStruct((members, cap, lanes), jnp.bfloat16),
        ),
        in_specs=[vmem, smem, vmem],
        out_specs=(pl.BlockSpec(memory_space=pl.ANY), vmem),
        scratch_shapes=[pltpu.VMEM((BUCKET + 8, lanes), jnp.float32), dma((4,))],
    )(avg, lane_slots, back)
    return averaged, returned[None]


def solution(mesh):
    return jax.shard_map(
        functools.partial(per_device, mesh.shape["grp"], mesh.shape["mem"]),
        mesh=mesh,
        in_specs=(
            P(("grp", "mem"), None, None, None),
            P(("grp", "mem"), None, None),
            P(("grp", "mem"), None),
        ),
        out_specs=(P("mem", None), P(("grp", "mem"), None, None, None)),
        check_vma=False,
    )
```

time: 169 us -> 28.7 us (0.17)
  waiting for transfers between devices: 83.5 us -> 0 us
  blocking collectives: 28 us -> 0 us
  Pallas kernels: 0 us -> 27.9 us
  other arithmetic: 16.1 us -> 0 us
  between operations: 14.1 us -> 0.64 us
  starting transfers between devices: 9.75 us -> 0 us
  local copies, waits for them, and re-layouts: 8.36 us -> 0 us
  matrix products: 8.07 us -> 0 us
    psum x1 -> x0, waiting for transfers between devices: 74.6 us -> none  [per_device(): reduced = lax.psum(payload, 'grp')]
    pallas_call x0 -> x2, Pallas kernels: none -> 27.9 us  [the longest x1 20.8 us: per_device(): pl.pallas_call(functools.partial(exchange_kernel, groups, members, cap),...]
    psum x1 -> x0, blocking collectives: 17.7 us -> none  [per_device(): reduced = lax.psum(payload, 'grp')]
    all_to_all x1 -> x0, blocking collectives: 10.3 us -> none  [per_device(): lax.all_to_all(back_rows, 'mem', split_axis=0, concat_axis=0, tiled=True)]
    all_to_all x2 -> x0, starting transfers between devices: 9.71 us -> none  [the longest x1 6.35 us: per_device(): lax.all_to_all(send_slots, 'mem', split_axis=0, concat_axis=0, tiled=True)]
    all_to_all x2 -> x0, waiting for transfers between devices: 8.91 us -> none  [the longest x1 5.7 us: per_device(): lax.all_to_all(send_blocks, 'mem', split_axis=0, concat_axis=0, tiled=True)]
    dot_general x7 -> x0, matrix products: 8.07 us -> none  [one_tile(): return jnp.dot(onehot, rows_in, preferred_element_type=jnp.float32)]
    div x1 -> x0, other arithmetic: 5.72 us -> none  [per_device(): averaged = reduced[0] / jnp.maximum(total_count, 1.0)[:, None]]
  transfers between devices with their start and end apart: 3 -> 0, of which waited for: 3 -> 0; matrix products, arithmetic and copies ran while one was open for 3% -> 0% of each run, Pallas kernels for 0% -> 0%
where the time goes in v1:
time: 28.7 us; the launch traced here: 28.6 us
  Pallas kernels  27.9 us (97%)
  between operations  0.64 us (2%)
    pallas_call x1, Pallas kernels, per_device(): pl.pallas_call(functools.partial(exchange_kernel, groups, members, cap),...  20.8 us
    pallas_call x1, Pallas kernels, per_device(): pl.pallas_call(functools.partial(place_kernel, total), out_shape=(jax.Sha...  7.09 us

profile of v1, /device:TPU:0, one launch (start us, length us, event | category | flops | bytes accessed | tf_op | source)
XLA Modules:
  0.0 28.6 jit_solution(16717335564341766868)
XLA Ops:
  0.6 20.8 %shard_map.50 = (f32[1024,128]{1,0:T(8,128)}, s32[8,128]{1,0:T(8,128)}, bf16[8,32,128]{2,1,0:T(8,128)(2,1)}) custom-call(bf16[1,8,32,128]{3,2,1,0:T(8,128)(2,1)} %values_ref.1, s32[1,8,32]{2,1,0:T(8,128)} %slots_ref.1, s32[1,8]{1,0:T(1,128)} %counts_ref.1), custom_call_target="tpu_custom_call" | custom-call | tf_op jit(solution)/shard_map/pallas_call | solution.py:278
  21.5 7.1 %shard_map.51 = (f32[7168,128]{1,0:T(8,128)}, bf16[8,32,128]{2,1,0:T(8,128)(2,1)}) custom-call(f32[1024,128]{1,0:T(8,128)} %get-tuple-element.7.avg_ref, s32[8,128]{1,0:T(8,128)} %get-tuple-element.8.slot_ref, bf16[8,32,128]{2,1,0:T(8,128)(2,1)} %get-tuple-element.9.back_ref), custom_call_target="tpu_custom_call" | custom-call | tf_op jit(solution)/shard_map/pallas_call | solution.py:300

commit v2 on v1

v2 whole, which is shorter than its diff:
```python
import functools

import jax
import jax.numpy as jnp
from jax import lax
from jax.experimental import pallas as pl
from jax.experimental.pallas import tpu as pltpu
from jax.sharding import PartitionSpec as P

BUCKET = 7168
LANES = 128
ROWS = 256
WIDE = 1024
EXTRA = 8


def exchange_kernel(
    groups, members, cap,
    values_ref, slots_ref, counts_ref,
    avg_ref, lane_ref, back_ref,
    got, pay, slots_v, counts_s, lane_i, lane_f, avg_v, ret,
    v_send, v_recv, f_send, f_recv, r_send, r_recv, local_sem, avg_sem,
):
    g = lax.axis_index("grp")
    m = lax.axis_index("mem")
    total = groups * members * cap
    per_row = LANES // cap

    def each(low, high, body):
        if high - low <= 8:
            for k in range(low, high):
                body(k)
        else:
            lax.fori_loop(low, high, lambda k, c: (body(k), c)[1], 0)

    barrier = pltpu.get_barrier_semaphore()
    for step in range(1, members):
        pl.semaphore_signal(barrier, inc=1, device_id={"mem": lax.rem(m + step, members)})
    for step in range(1, groups):
        pl.semaphore_signal(barrier, inc=1, device_id={"grp": lax.rem(g + step, groups)})

    load_v = pltpu.make_async_copy(values_ref.at[0], pay.at[:, pl.ds(0, cap), :], local_sem.at[0])
    load_s = pltpu.make_async_copy(slots_ref.at[0], slots_v, local_sem.at[1])
    load_c = pltpu.make_async_copy(counts_ref, counts_s, local_sem.at[2])
    load_c.start()
    load_s.start()
    load_v.start()
    load_c.wait()
    load_s.wait()

    raw = slots_v[...]
    shown = jnp.concatenate([raw] * per_row, axis=1)
    row_id = lax.broadcasted_iota(jnp.int32, (members, LANES), 0)
    entry = lax.rem(lax.broadcasted_iota(jnp.int32, (members, LANES), 1), cap)
    limit = jnp.zeros((members, LANES), jnp.int32)
    for k in range(members):
        limit = jnp.where(row_id == k, counts_s[0, k], limit)
    masked = jnp.where(entry < limit, shown, -LANES)
    high = (masked >> 7).astype(jnp.float32)
    low = (masked & (LANES - 1)).astype(jnp.float32)
    part_id = lax.broadcasted_iota(jnp.int32, (EXTRA, LANES), 0)
    for k in range(members):
        both = jnp.where(part_id == 0, high[k : k + 1, :], low[k : k + 1, :])
        pay[k, cap:, :] = both.astype(jnp.bfloat16)
    load_v.wait()

    pl.semaphore_wait(barrier, members - 1 + groups - 1)

    mine = g * members + m

    def to_member(step):
        peer = lax.rem(m + step, members)
        return pltpu.make_async_remote_copy(
            pay.at[peer], got.at[mine], v_send.at[step], v_recv.at[step],
            device_id={"mem": peer},
        )

    def from_member(step):
        src = lax.rem(m + members - step, members)
        return pltpu.make_async_remote_copy(
            pay.at[src], got.at[g * members + src], v_send.at[step], v_recv.at[step],
            device_id={"mem": src},
        )

    def to_group(step, hop):
        src = lax.rem(m + members - step, members)
        at = g * members + src
        return pltpu.make_async_remote_copy(
            got.at[at], got.at[at], f_send.at[step, hop], f_recv.at[step, hop],
            device_id={"grp": lax.rem(g + hop, groups)},
        )

    def from_group(step, hop):
        src = lax.rem(m + members - step, members)
        peer = lax.rem(g + groups - hop, groups)
        at = peer * members + src
        return pltpu.make_async_remote_copy(
            got.at[at], got.at[at], f_send.at[step, hop], f_recv.at[step, hop],
            device_id={"grp": peer},
        )

    local_v = pltpu.make_async_copy(pay.at[m], got.at[mine], local_sem.at[0])
    local_v.start()
    each(1, members, lambda step: to_member(step).start())
    local_v.wait()

    def forward(step):
        for hop in range(1, groups):
            to_group(step, hop).start()

    forward(0)

    def pass_on(step):
        from_member(step).wait_recv()
        forward(step)

    each(1, members, pass_on)

    def land(step):
        for hop in range(1, groups):
            from_group(step, hop).wait_recv()

    each(0, members, land)

    lane = lax.broadcasted_iota(jnp.int32, (1, LANES), 1)

    def slots_of(sender):
        halves = got[sender, pl.ds(cap, EXTRA), :].astype(jnp.float32)
        return halves[0:1, :] * float(LANES) + halves[1:2, :]

    def pack(k):
        row = slots_of(k * per_row)
        for q in range(1, per_row):
            row = jnp.where(lane >= q * cap, slots_of(k * per_row + q), row)
        lane_i[pl.ds(k, 1), :] = jnp.where(row < 0, float(BUCKET), row).astype(jnp.int32)
        lane_f[pl.ds(k, 1), :] = row

    each(0, total // LANES, pack)
    store_lane = pltpu.make_async_copy(lane_i, lane_ref, local_sem.at[1])
    store_lane.start()

    wide = min(WIDE, total)
    senders_wide = wide // cap
    halves = ROWS // LANES

    def block(b):
        columns = []
        for h in range(halves):
            row = lane_f[pl.ds(b * halves + h, 1), :]
            row = jnp.where(row < 0, -2.0, row)
            columns.append(jnp.transpose(jnp.broadcast_to(row, (LANES, LANES))))
        column = jnp.concatenate(columns, axis=0)

        def part(w):
            same = []
            for l in range(wide // LANES):
                row = lane_f[pl.ds(w * (wide // LANES) + l, 1), :]
                same.append(jnp.where(column == row, 1.0, 0.0).astype(jnp.bfloat16))
            onehot = jnp.concatenate(same, axis=1)
            rows = got[pl.ds(w * senders_wide, senders_wide), :cap, :].reshape(wide, LANES)
            rows = jnp.concatenate([rows, jnp.ones((wide, LANES), jnp.bfloat16)], axis=1)
            return jnp.dot(onehot, rows, preferred_element_type=jnp.float32)

        if total == wide:
            acc = part(0)
        else:
            acc = lax.fori_loop(
                0, total // wide, lambda w, a: a + part(w), jnp.zeros((ROWS, 2 * LANES), jnp.float32)
            )
        avg = acc[:, :LANES] / jnp.maximum(acc[:, LANES:], 1.0)
        avg_v[pl.ds(b * ROWS, ROWS), :] = avg
        return avg

    def store_avg(q):
        at = pl.ds(lax.rem(g + q, groups) * members * cap, members * cap)
        return pltpu.make_async_copy(avg_v.at[at], avg_ref.at[at], avg_sem.at[q])

    blocks_each = members * cap // ROWS
    senders_each = ROWS // cap

    def own_block(t):
        avg = block(g * blocks_each + t)
        ret[pl.ds(t * senders_each, senders_each)] = avg.astype(jnp.bfloat16).reshape(
            senders_each, cap, LANES
        )

    each(0, blocks_each, own_block)

    def back_to(step):
        peer = lax.rem(m + step, members)
        return pltpu.make_async_remote_copy(
            ret.at[peer], back_ref.at[m], r_send.at[step], r_recv.at[step],
            device_id={"mem": peer},
        )

    def back_from(step):
        src = lax.rem(m + members - step, members)
        return pltpu.make_async_remote_copy(
            ret.at[src], back_ref.at[src], r_send.at[step], r_recv.at[step],
            device_id={"mem": src},
        )

    each(1, members, lambda step: back_to(step).start())
    local_r = pltpu.make_async_copy(ret.at[m], back_ref.at[m], local_sem.at[2])
    local_r.start()
    store_avg(0).start()

    for q in range(1, groups):
        other = lax.rem(g + q, groups)
        each(0, blocks_each, lambda t, other=other: (block(other * blocks_each + t), None)[1])
        store_avg(q).start()

    def finish_forward(step):
        for hop in range(1, groups):
            to_group(step, hop).wait_send()

    each(0, members, finish_forward)
    each(1, members, lambda step: to_member(step).wait_send())
    store_lane.wait()
    for q in range(groups):
        store_avg(q).wait()
    local_r.wait()
    each(1, members, lambda step: back_to(step).wait_send())
    each(1, members, lambda step: back_from(step).wait_recv())


def place_kernel(total, avg_ref, slot_ref, back_ref, out_ref, returned_ref, table, rows, slot_s, back_v, in_sem, sems):
    unroll = 32
    load_s = pltpu.make_async_copy(slot_ref, slot_s, in_sem.at[0])
    load_a = pltpu.make_async_copy(avg_ref, rows, in_sem.at[1])
    load_b = pltpu.make_async_copy(back_ref, back_v, in_sem.at[2])
    store_b = pltpu.make_async_copy(back_v, returned_ref, in_sem.at[3])
    load_s.start()
    load_a.start()
    load_b.start()
    table[...] = jnp.zeros_like(table)
    load_s.wait()
    load_a.wait()
    load_b.wait()
    store_b.start()

    def step(i, carry):
        base = pl.multiple_of(i * unroll, unroll)
        row = base // LANES
        col = lax.rem(base, LANES)
        for k in range(unroll):
            s = slot_s[row, col + k]
            table[pl.ds(s, 1), :] = rows[pl.ds(base + k, 1), :]
        return carry

    lax.fori_loop(0, total // unroll, step, 0)
    pieces = sems.shape[0]
    size = BUCKET // pieces
    copies = [
        pltpu.make_async_copy(
            table.at[pl.ds(k * size, size)], out_ref.at[pl.ds(k * size, size)], sems.at[k]
        )
        for k in range(pieces)
    ]
    for copy in copies:
        copy.start()
    store_b.wait()
    for copy in copies:
        copy.wait()


def per_device(groups, members, values, slots, counts):
    cap, lanes = values.shape[2:]
    total = groups * members * cap
    hbm = pl.BlockSpec(memory_space=pl.ANY)
    dma = pltpu.SemaphoreType.DMA
    avg, lane_slots, back = pl.pallas_call(
        functools.partial(exchange_kernel, groups, members, cap),
        out_shape=(
            jax.ShapeDtypeStruct((total, lanes), jnp.float32),
            jax.ShapeDtypeStruct((total // LANES, LANES), jnp.int32),
            jax.ShapeDtypeStruct((members, cap, lanes), jnp.bfloat16),
        ),
        in_specs=[hbm, hbm, hbm],
        out_specs=(hbm, hbm, hbm),
        scratch_shapes=[
            pltpu.VMEM((groups * members, cap + EXTRA, lanes), jnp.bfloat16),
            pltpu.VMEM((members, cap + EXTRA, lanes), jnp.bfloat16),
            pltpu.VMEM((members, cap), jnp.int32),
            pltpu.SMEM((1, members), jnp.int32),
            pltpu.VMEM((total // LANES, LANES), jnp.int32),
            pltpu.VMEM((total // LANES, LANES), jnp.float32),
            pltpu.VMEM((total, lanes), jnp.float32),
            pltpu.VMEM((members, cap, lanes), jnp.bfloat16),
            dma((members,)), dma((members,)),
            dma((members, groups)), dma((members, groups)),
            dma((members,)), dma((members,)), dma((3,)), dma((groups,)),
        ],
        compiler_params=pltpu.CompilerParams(collective_id=0, has_side_effects=True),
    )(values, slots, counts)
    averaged, returned = pl.pallas_call(
        functools.partial(place_kernel, total),
        out_shape=(
            jax.ShapeDtypeStruct((BUCKET, lanes), jnp.float32),
            jax.ShapeDtypeStruct((members, cap, lanes), jnp.bfloat16),
        ),
        in_specs=[hbm, hbm, hbm],
        out_specs=(hbm, hbm),
        scratch_shapes=[
            pltpu.VMEM((BUCKET + 8, lanes), jnp.float32),
            pltpu.VMEM((total, lanes), jnp.float32),
            pltpu.SMEM((total // LANES, LANES), jnp.int32),
            pltpu.VMEM((members, cap, lanes), jnp.bfloat16),
            dma((4,)), dma((8,)),
        ],
    )(avg, lane_slots, back)
    return averaged, returned[None]


def solution(mesh):
    return jax.shard_map(
        functools.partial(per_device, mesh.shape["grp"], mesh.shape["mem"]),
        mesh=mesh,
        in_specs=(
            P(("grp", "mem"), None, None, None),
            P(("grp", "mem"), None, None),
            P(("grp", "mem"), None),
        ),
        out_specs=(P("mem", None), P(("grp", "mem"), None, None, None)),
        check_vma=False,
    )
```

time: 28.7 us -> 24.8 us (0.86)
  Pallas kernels: 27.9 us -> 24 us
    pallas_call x1, Pallas kernels: 20.8 us -> 18.6 us  [per_device(): pl.pallas_call(functools.partial(exchange_kernel, groups, members, cap),...]
    pallas_call x1, Pallas kernels: 7.09 us -> 5.41 us  [per_device(): pl.pallas_call(functools.partial(place_kernel, total), out_shape=(jax.Sha...]
where the time goes in v2:
time: 24.8 us; the launch traced here: 24.7 us
  Pallas kernels  24 us (97%)
  between operations  0.64 us (3%)
    pallas_call x1, Pallas kernels, per_device(): pl.pallas_call(functools.partial(exchange_kernel, groups, members, cap),...  18.6 us
    pallas_call x1, Pallas kernels, per_device(): pl.pallas_call(functools.partial(place_kernel, total), out_shape=(jax.Sha...  5.41 us

profile of v2, /device:TPU:0, one launch (start us, length us, event | category | flops | bytes accessed | tf_op | source)
XLA Modules:
  0.0 24.7 jit_solution(8490936110762788453)
XLA Ops:
  0.6 18.6 %shard_map.50 = (f32[1024,128]{1,0:T(8,128)}, s32[8,128]{1,0:T(8,128)}, bf16[8,32,128]{2,1,0:T(8,128)(2,1)}) custom-call(bf16[1,8,32,128]{3,2,1,0:T(8,128)(2,1)} %values_ref.1, s32[1,8,32]{2,1,0:T(8,128)} %slots_ref.1, s32[1,8]{1,0:T(1,128)} %counts_ref.1), custom_call_target="tpu_custom_call" | custom-call | tf_op jit(solution)/shard_map/pallas_call | solution.py:272
  19.3 5.4 %shard_map.51 = (f32[7168,128]{1,0:T(8,128)}, bf16[8,32,128]{2,1,0:T(8,128)(2,1)}) custom-call(f32[1024,128]{1,0:T(8,128)} %get-tuple-element.7.avg_ref, s32[8,128]{1,0:T(8,128)} %get-tuple-element.8.slot_ref, bf16[8,32,128]{2,1,0:T(8,128)(2,1)} %get-tuple-element.9.back_ref), custom_call_target="tpu_custom_call" | custom-call | tf_op jit(solution)/shard_map/pallas_call | solution.py:296

commit v3 on v2

--- a/solution.py
+++ b/solution.py
@@ -11,15 +11,36 @@
 LANES = 128
 ROWS = 256
 WIDE = 1024
-EXTRA = 8
+
+
+def partner(index, step, count):
+    if count & (count - 1):
+        return None
+    bit = 1
+    while bit < count:
+        flip = (step // bit) % 2
+        index = index + flip * bit * (1 - 2 * ((index // bit) % 2))
+        bit *= 2
+    return index
+
+
+def target(index, step, count):
+    paired = partner(index, step, count)
+    return lax.rem(index + step, count) if paired is None else paired
+
+
+def origin(index, step, count):
+    paired = partner(index, step, count)
+    return lax.rem(index + count - step, count) if paired is None else paired
 
 
 def exchange_kernel(
     groups, members, cap,
     values_ref, slots_ref, counts_ref,
     avg_ref, lane_ref, back_ref,
-    got, pay, slots_v, counts_s, lane_i, lane_f, avg_v, ret,
-    v_send, v_recv, f_send, f_recv, r_send, r_recv, local_sem, avg_sem,
+    got, got_slots, vals, own_slots, slots_v, counts_s, lane_i, lane_f, same_v, avg_v, ret,
+    v_send, v_recv, s_send, s_recv, f_send, f_recv, fs_send, fs_recv,
+    r_send, r_recv, local_sem, avg_sem,
 ):
     g = lax.axis_index("grp")
     m = lax.axis_index("mem")
@@ -39,7 +60,7 @@
     for step in range(1, groups):
         pl.semaphore_signal(barrier, inc=1, device_id={"grp": lax.rem(g + step, groups)})
 
-    load_v = pltpu.make_async_copy(values_ref.at[0], pay.at[:, pl.ds(0, cap), :], local_sem.at[0])
+    load_v = pltpu.make_async_copy(values_ref.at[0], vals, local_sem.at[0])
     load_s = pltpu.make_async_copy(slots_ref.at[0], slots_v, local_sem.at[1])
     load_c = pltpu.make_async_copy(counts_ref, counts_s, local_sem.at[2])
     load_c.start()
@@ -55,54 +76,81 @@
     limit = jnp.zeros((members, LANES), jnp.int32)
     for k in range(members):
         limit = jnp.where(row_id == k, counts_s[0, k], limit)
-    masked = jnp.where(entry < limit, shown, -LANES)
-    high = (masked >> 7).astype(jnp.float32)
-    low = (masked & (LANES - 1)).astype(jnp.float32)
-    part_id = lax.broadcasted_iota(jnp.int32, (EXTRA, LANES), 0)
+    masked = jnp.where(entry < limit, shown, -1)
     for k in range(members):
-        both = jnp.where(part_id == 0, high[k : k + 1, :], low[k : k + 1, :])
-        pay[k, cap:, :] = both.astype(jnp.bfloat16)
+        own_slots[k] = masked[k : k + 1, :]
     load_v.wait()
 
     pl.semaphore_wait(barrier, members - 1 + groups - 1)
 
     mine = g * members + m
 
+    def slots_to(step):
+        peer = target(m, step, members)
+        return pltpu.make_async_remote_copy(
+            own_slots.at[peer], got_slots.at[mine], s_send.at[step], s_recv.at[step],
+            device_id={"mem": peer},
+        )
+
+    def slots_from(step):
+        src = origin(m, step, members)
+        return pltpu.make_async_remote_copy(
+            own_slots.at[src], got_slots.at[g * members + src], s_send.at[step], s_recv.at[step],
+            device_id={"mem": src},
+        )
+
     def to_member(step):
-        peer = lax.rem(m + step, members)
-        return pltpu.make_async_remote_copy(
-            pay.at[peer], got.at[mine], v_send.at[step], v_recv.at[step],
+        peer = target(m, step, members)
+        return pltpu.make_async_remote_copy(
+            vals.at[peer], got.at[mine], v_send.at[step], v_recv.at[step],
             device_id={"mem": peer},
         )
 
     def from_member(step):
-        src = lax.rem(m + members - step, members)
-        return pltpu.make_async_remote_copy(
-            pay.at[src], got.at[g * members + src], v_send.at[step], v_recv.at[step],
+        src = origin(m, step, members)
+        return pltpu.make_async_remote_copy(
+            vals.at[src], got.at[g * members + src], v_send.at[step], v_recv.at[step],
             device_id={"mem": src},
         )
 
     def to_group(step, hop):
-        src = lax.rem(m + members - step, members)
-        at = g * members + src
+        at = g * members + origin(m, step, members)
         return pltpu.make_async_remote_copy(
             got.at[at], got.at[at], f_send.at[step, hop], f_recv.at[step, hop],
-            device_id={"grp": lax.rem(g + hop, groups)},
+            device_id={"grp": target(g, hop, groups)},
         )
 
     def from_group(step, hop):
-        src = lax.rem(m + members - step, members)
-        peer = lax.rem(g + groups - hop, groups)
-        at = peer * members + src
+        peer = origin(g, hop, groups)
+        at = peer * members + origin(m, step, members)
         return pltpu.make_async_remote_copy(
             got.at[at], got.at[at], f_send.at[step, hop], f_recv.at[step, hop],
             device_id={"grp": peer},
         )
 
-    local_v = pltpu.make_async_copy(pay.at[m], got.at[mine], local_sem.at[0])
+    def slots_to_group(hop):
+        at = pl.ds(g * members, members)
+        return pltpu.make_async_remote_copy(
+            got_slots.at[at], got_slots.at[at], fs_send.at[hop], fs_recv.at[hop],
+            device_id={"grp": target(g, hop, groups)},
+        )
+
+    def slots_from_group(hop):
+        peer = origin(g, hop, groups)
+        at = pl.ds(peer * members, members)
+        return pltpu.make_async_remote_copy(
+            got_slots.at[at], got_slots.at[at], fs_send.at[hop], fs_recv.at[hop],
+            device_id={"grp": peer},
+        )
+
+    local_v = pltpu.make_async_copy(vals.at[m], got.at[mine], local_sem.at[0])
+    local_s = pltpu.make_async_copy(own_slots.at[m], got_slots.at[mine], local_sem.at[2])
     local_v.start()
+    local_s.start()
+    each(1, members, lambda step: slots_to(step).start())
     each(1, members, lambda step: to_member(step).start())
     local_v.wait()
+    local_s.wait()
 
     def forward(step):
         for hop in range(1, groups):
@@ -114,26 +162,23 @@
         from_member(step).wait_recv()
         forward(step)
 
-    each(1, members, pass_on)
-
-    def land(step):
-        for hop in range(1, groups):
-            from_group(step, hop).wait_recv()
-
-    each(0, members, land)
+    early = members - members // 4
+    each(1, early, pass_on)
+    each(1, members, lambda step: slots_from(step).wait_recv())
+    for hop in range(1, groups):
+        slots_to_group(hop).start()
+    each(early, members, pass_on)
+    for hop in range(1, groups):
+        slots_from_group(hop).wait_recv()
 
     lane = lax.broadcasted_iota(jnp.int32, (1, LANES), 1)
 
-    def slots_of(sender):
-        halves = got[sender, pl.ds(cap, EXTRA), :].astype(jnp.float32)
-        return halves[0:1, :] * float(LANES) + halves[1:2, :]
-
     def pack(k):
-        row = slots_of(k * per_row)
+        row = got_slots[k * per_row]
         for q in range(1, per_row):
-            row = jnp.where(lane >= q * cap, slots_of(k * per_row + q), row)
-        lane_i[pl.ds(k, 1), :] = jnp.where(row < 0, float(BUCKET), row).astype(jnp.int32)
-        lane_f[pl.ds(k, 1), :] = row
+            row = jnp.where(lane >= q * cap, got_slots[k * per_row + q], row)
+        lane_i[pl.ds(k, 1), :] = jnp.where(row < 0, BUCKET, row)
+        lane_f[pl.ds(k, 1), :] = row.astype(jnp.float32)
 
     each(0, total // LANES, pack)
     store_lane = pltpu.make_async_copy(lane_i, lane_ref, local_sem.at[1])
@@ -143,34 +188,42 @@
     senders_wide = wide // cap
     halves = ROWS // LANES
 
-    def block(b):
+    def column_of(b):
         columns = []
         for h in range(halves):
             row = lane_f[pl.ds(b * halves + h, 1), :]
             row = jnp.where(row < 0, -2.0, row)
             columns.append(jnp.transpose(jnp.broadcast_to(row, (LANES, LANES))))
-        column = jnp.concatenate(columns, axis=0)
-
-        def part(w):
-            same = []
-            for l in range(wide // LANES):
-                row = lane_f[pl.ds(w * (wide // LANES) + l, 1), :]
-                same.append(jnp.where(column == row, 1.0, 0.0).astype(jnp.bfloat16))
-            onehot = jnp.concatenate(same, axis=1)
-            rows = got[pl.ds(w * senders_wide, senders_wide), :cap, :].reshape(wide, LANES)
-            rows = jnp.concatenate([rows, jnp.ones((wide, LANES), jnp.bfloat16)], axis=1)
-            return jnp.dot(onehot, rows, preferred_element_type=jnp.float32)
-
+        return jnp.concatenate(columns, axis=0)
+
+    def same_part(column, w):
+        same = []
+        for l in range(wide // LANES):
+            row = lane_f[pl.ds(w * (wide // LANES) + l, 1), :]
+            same.append(jnp.where(column == row, 1.0, 0.0).astype(jnp.bfloat16))
+        return jnp.concatenate(same, axis=1)
+
+    def sum_part(same, w):
+        rows = got[pl.ds(w * senders_wide, senders_wide)].reshape(wide, LANES)
+        rows = jnp.concatenate([rows, jnp.ones((wide, LANES), jnp.bfloat16)], axis=1)
+        return jnp.dot(same, rows, preferred_element_type=jnp.float32)
+
+    def average(b, same_of):
         if total == wide:
-            acc = part(0)
+            acc = sum_part(same_of(0), 0)
         else:
             acc = lax.fori_loop(
-                0, total // wide, lambda w, a: a + part(w), jnp.zeros((ROWS, 2 * LANES), jnp.float32)
+                0, total // wide, lambda w, a: a + sum_part(same_of(w), w),
+                jnp.zeros((ROWS, 2 * LANES), jnp.float32),
             )
         avg = acc[:, :LANES] / jnp.maximum(acc[:, LANES:], 1.0)
         avg_v[pl.ds(b * ROWS, ROWS), :] = avg
         return avg
 
+    def block(b):
+        column = column_of(b)
+        return average(b, lambda w: same_part(column, w))
+
     def store_avg(q):
         at = pl.ds(lax.rem(g + q, groups) * members * cap, members * cap)
         return pltpu.make_async_copy(avg_v.at[at], avg_ref.at[at], avg_sem.at[q])
@@ -178,8 +231,19 @@
     blocks_each = members * cap // ROWS
     senders_each = ROWS // cap
 
+    held = blocks_each == 1 and total == wide
+    if held:
+        same_v[...] = same_part(column_of(g), 0)
+
+    def land(step):
+        for hop in range(1, groups):
+            from_group(step, hop).wait_recv()
+
+    each(0, members, land)
+
     def own_block(t):
-        avg = block(g * blocks_each + t)
+        b = g * blocks_each + t
+        avg = average(b, lambda w: same_v[...]) if held else block(b)
         ret[pl.ds(t * senders_each, senders_each)] = avg.astype(jnp.bfloat16).reshape(
             senders_each, cap, LANES
         )
@@ -187,20 +251,20 @@
     each(0, blocks_each, own_block)
 
     def back_to(step):
-        peer = lax.rem(m + step, members)
+        peer = target(m, step, members)
         return pltpu.make_async_remote_copy(
             ret.at[peer], back_ref.at[m], r_send.at[step], r_recv.at[step],
             device_id={"mem": peer},
         )
 
     def back_from(step):
-        src = lax.rem(m + members - step, members)
+        src = origin(m, step, members)
         return pltpu.make_async_remote_copy(
             ret.at[src], back_ref.at[src], r_send.at[step], r_recv.at[step],
             device_id={"mem": src},
         )
 
-    each(1, members, lambda step: back_to(step).start())
+    each(1, members, lambda step: back_to(members - step).start())
     local_r = pltpu.make_async_copy(ret.at[m], back_ref.at[m], local_sem.at[2])
     local_r.start()
     store_avg(0).start()
@@ -215,7 +279,9 @@
             to_group(step, hop).wait_send()
 
     each(0, members, finish_forward)
-    each(1, members, lambda step: to_member(step).wait_send())
+    each(1, members, lambda step: (to_member(step).wait_send(), slots_to(step).wait_send())[0])
+    for hop in range(1, groups):
+        slots_to_group(hop).wait_send()
     store_lane.wait()
     for q in range(groups):
         store_avg(q).wait()
@@ -279,16 +345,19 @@
         in_specs=[hbm, hbm, hbm],
         out_specs=(hbm, hbm, hbm),
         scratch_shapes=[
-            pltpu.VMEM((groups * members, cap + EXTRA, lanes), jnp.bfloat16),
-            pltpu.VMEM((members, cap + EXTRA, lanes), jnp.bfloat16),
+            pltpu.VMEM((groups * members, cap, lanes), jnp.bfloat16),
+            pltpu.VMEM((groups * members, 1, LANES), jnp.int32),
+            pltpu.VMEM((members, cap, lanes), jnp.bfloat16),
+            pltpu.VMEM((members, 1, LANES), jnp.int32),
             pltpu.VMEM((members, cap), jnp.int32),
             pltpu.SMEM((1, members), jnp.int32),
             pltpu.VMEM((total // LANES, LANES), jnp.int32),
             pltpu.VMEM((total // LANES, LANES), jnp.float32),
+            pltpu.VMEM((ROWS, min(WIDE, total)), jnp.bfloat16),
             pltpu.VMEM((total, lanes), jnp.float32),
             pltpu.VMEM((members, cap, lanes), jnp.bfloat16),
-            dma((members,)), dma((members,)),
-            dma((members, groups)), dma((members, groups)),
+            dma((members,)), dma((members,)), dma((members,)), dma((members,)),
+            dma((members, groups)), dma((members, groups)), dma((groups,)), dma((groups,)),
             dma((members,)), dma((members,)), dma((3,)), dma((groups,)),
         ],
         compiler_params=pltpu.CompilerParams(collective_id=0, has_side_effects=True),

time: 24.8 us -> 24.9 us (level)
  no operation moved by 1% of the time
where the time goes in v3:
time: 24.9 us; the launch traced here: 24.7 us
  Pallas kernels  24.1 us (97%)
  between operations  0.64 us (3%)
    pallas_call x1, Pallas kernels, per_device(): pl.pallas_call(functools.partial(exchange_kernel, groups, members, cap),...  18.7 us
    pallas_call x1, Pallas kernels, per_device(): pl.pallas_call(functools.partial(place_kernel, total), out_shape=(jax.Sha...  5.41 us

profile of v3, /device:TPU:0, one launch (start us, length us, event | category | flops | bytes accessed | tf_op | source)
XLA Modules:
  0.0 24.7 jit_solution(8032501397692354588)
XLA Ops:
  0.6 18.7 %shard_map.50 = (f32[1024,128]{1,0:T(8,128)}, s32[8,128]{1,0:T(8,128)}, bf16[8,32,128]{2,1,0:T(8,128)(2,1)}) custom-call(bf16[1,8,32,128]{3,2,1,0:T(8,128)(2,1)} %values_ref.1, s32[1,8,32]{2,1,0:T(8,128)} %slots_ref.1, s32[1,8]{1,0:T(1,128)} %counts_ref.1), custom_call_target="tpu_custom_call" | custom-call | tf_op jit(solution)/shard_map/pallas_call | solution.py:338
  19.3 5.4 %shard_map.51 = (f32[7168,128]{1,0:T(8,128)}, bf16[8,32,128]{2,1,0:T(8,128)(2,1)}) custom-call(f32[1024,128]{1,0:T(8,128)} %get-tuple-element.7.avg_ref, s32[8,128]{1,0:T(8,128)} %get-tuple-element.8.slot_ref, bf16[8,32,128]{2,1,0:T(8,128)(2,1)} %get-tuple-element.9.back_ref), custom_call_target="tpu_custom_call" | custom-call | tf_op jit(solution)/shard_map/pallas_call | solution.py:365

commit v4 on v3

--- a/solution.py
+++ b/solution.py
@@ -38,7 +38,7 @@
     groups, members, cap,
     values_ref, slots_ref, counts_ref,
     avg_ref, lane_ref, back_ref,
-    got, got_slots, vals, own_slots, slots_v, counts_s, lane_i, lane_f, same_v, avg_v, ret,
+    got, got_slots, vals, own_slots, slots_v, counts_s, lane_i, lane_f, full_f, rank_f, halves_v, same_v, avg_v, ret,
     v_send, v_recv, s_send, s_recv, f_send, f_recv, fs_send, fs_recv,
     r_send, r_recv, local_sem, avg_sem,
 ):
@@ -177,12 +177,11 @@
         row = got_slots[k * per_row]
         for q in range(1, per_row):
             row = jnp.where(lane >= q * cap, got_slots[k * per_row + q], row)
-        lane_i[pl.ds(k, 1), :] = jnp.where(row < 0, BUCKET, row)
         lane_f[pl.ds(k, 1), :] = row.astype(jnp.float32)
+        full_f[pl.ds(k, 1), :] = jnp.where(row < 0, BUCKET, row).astype(jnp.float32)
 
     each(0, total // LANES, pack)
     store_lane = pltpu.make_async_copy(lane_i, lane_ref, local_sem.at[1])
-    store_lane.start()
 
     wide = min(WIDE, total)
     senders_wide = wide // cap
@@ -191,8 +190,7 @@
     def column_of(b):
         columns = []
         for h in range(halves):
-            row = lane_f[pl.ds(b * halves + h, 1), :]
-            row = jnp.where(row < 0, -2.0, row)
+            row = full_f[pl.ds(b * halves + h, 1), :]
             columns.append(jnp.transpose(jnp.broadcast_to(row, (LANES, LANES))))
         return jnp.concatenate(columns, axis=0)
 
@@ -208,7 +206,7 @@
         rows = jnp.concatenate([rows, jnp.ones((wide, LANES), jnp.bfloat16)], axis=1)
         return jnp.dot(same, rows, preferred_element_type=jnp.float32)
 
-    def average(b, same_of):
+    def average(same_of):
         if total == wide:
             acc = sum_part(same_of(0), 0)
         else:
@@ -216,17 +214,17 @@
                 0, total // wide, lambda w, a: a + sum_part(same_of(w), w),
                 jnp.zeros((ROWS, 2 * LANES), jnp.float32),
             )
-        avg = acc[:, :LANES] / jnp.maximum(acc[:, LANES:], 1.0)
-        avg_v[pl.ds(b * ROWS, ROWS), :] = avg
-        return avg
+        return acc[:, :LANES] / jnp.maximum(acc[:, LANES:], 1.0)
 
     def block(b):
         column = column_of(b)
-        return average(b, lambda w: same_part(column, w))
-
-    def store_avg(q):
-        at = pl.ds(lax.rem(g + q, groups) * members * cap, members * cap)
-        return pltpu.make_async_copy(avg_v.at[at], avg_ref.at[at], avg_sem.at[q])
+        return average(lambda w: same_part(column, w))
+
+    blocks = total // ROWS
+
+    def store_avg(b):
+        at = pl.ds(b * ROWS, ROWS)
+        return pltpu.make_async_copy(avg_v.at[at], avg_ref.at[at], avg_sem.at[b])
 
     blocks_each = members * cap // ROWS
     senders_each = ROWS // cap
@@ -243,7 +241,7 @@
 
     def own_block(t):
         b = g * blocks_each + t
-        avg = average(b, lambda w: same_v[...]) if held else block(b)
+        avg = average(lambda w: same_v[...]) if held else block(b)
         ret[pl.ds(t * senders_each, senders_each)] = avg.astype(jnp.bfloat16).reshape(
             senders_each, cap, LANES
         )
@@ -267,12 +265,73 @@
     each(1, members, lambda step: back_to(members - step).start())
     local_r = pltpu.make_async_copy(ret.at[m], back_ref.at[m], local_sem.at[2])
     local_r.start()
-    store_avg(0).start()
-
-    for q in range(1, groups):
-        other = lax.rem(g + q, groups)
-        each(0, blocks_each, lambda t, other=other: (block(other * blocks_each + t), None)[1])
-        store_avg(q).start()
+
+    def lay(b):
+        column = column_of(b)
+        high = jnp.floor(column * (1.0 / LANES))
+        both = jnp.concatenate([high, column - high * LANES], axis=1)
+        halves_v[pl.ds(b * ROWS, ROWS), :] = both.astype(jnp.bfloat16)
+
+    each(0, blocks, lay)
+    lines = wide // LANES
+    down = lax.broadcasted_iota(jnp.int32, (ROWS, LANES), 0)
+
+    def rank(w):
+        keys = [
+            full_f[pl.ds(w * lines + l, 1), :].astype(jnp.int32) * total + (w * lines + l) * LANES + lane
+            for l in range(lines)
+        ]
+
+        def add(b, acc):
+            both = halves_v[pl.ds(b * ROWS, ROWS), :].astype(jnp.float32)
+            column = (both[:, :LANES] * float(LANES) + both[:, LANES:]).astype(jnp.int32)
+            column = column * total + (b * ROWS + down)
+            return tuple(
+                a + jnp.sum(jnp.where(column < key, 1.0, 0.0), axis=0, keepdims=True)
+                for a, key in zip(acc, keys)
+            )
+
+        acc = tuple(jnp.zeros((1, LANES), jnp.float32) for _ in range(lines))
+        if blocks <= 8:
+            for b in range(blocks):
+                acc = add(b, acc)
+        else:
+            acc = lax.fori_loop(0, blocks, add, acc)
+        for l in range(lines):
+            rank_f[pl.ds(w * lines + l, 1), :] = acc[l]
+
+    each(0, total // wide, rank)
+
+    def ordered(b):
+        place = (b * ROWS + down).astype(jnp.float32)
+
+        def pick(w):
+            chosen = jnp.concatenate(
+                [
+                    jnp.where(place == rank_f[pl.ds(w * lines + l, 1), :], 1.0, 0.0).astype(jnp.bfloat16)
+                    for l in range(lines)
+                ],
+                axis=1,
+            )
+            return jnp.dot(
+                chosen, halves_v[pl.ds(w * wide, wide), :], preferred_element_type=jnp.float32
+            )
+
+        if total == wide:
+            acc = pick(0)
+        else:
+            acc = lax.fori_loop(
+                0, total // wide, lambda w, a: a + pick(w), jnp.zeros((ROWS, 2 * LANES), jnp.float32)
+            )
+        column = acc[:, :LANES] * float(LANES) + acc[:, LANES:]
+        for h in range(halves):
+            turned = jnp.transpose(column[h * LANES : (h + 1) * LANES, :])
+            lane_i[pl.ds(b * halves + h, 1), :] = turned[0:1, :].astype(jnp.int32)
+        avg_v[pl.ds(b * ROWS, ROWS), :] = average(lambda w: same_part(column, w))
+        store_avg(b).start()
+
+    each(0, blocks, ordered)
+    store_lane.start()
 
     def finish_forward(step):
         for hop in range(1, groups):
@@ -283,8 +342,7 @@
     for hop in range(1, groups):
         slots_to_group(hop).wait_send()
     store_lane.wait()
-    for q in range(groups):
-        store_avg(q).wait()
+    each(0, blocks, lambda b: store_avg(b).wait())
     local_r.wait()
     each(1, members, lambda step: back_to(step).wait_send())
     each(1, members, lambda step: back_from(step).wait_recv())
@@ -305,26 +363,32 @@
     load_b.wait()
     store_b.start()
 
-    def step(i, carry):
+    chunks = total // unroll
+    pieces = sems.shape[0]
+    size = BUCKET // pieces
+
+    def more(bound, i):
+        at = jnp.minimum(i, chunks - 1) * unroll
+        return jnp.logical_and(i < chunks, slot_s[at // LANES, lax.rem(at, LANES)] < bound)
+
+    def step(i):
         base = pl.multiple_of(i * unroll, unroll)
         row = base // LANES
         col = lax.rem(base, LANES)
         for k in range(unroll):
             s = slot_s[row, col + k]
             table[pl.ds(s, 1), :] = rows[pl.ds(base + k, 1), :]
-        return carry
-
-    lax.fori_loop(0, total // unroll, step, 0)
-    pieces = sems.shape[0]
-    size = BUCKET // pieces
-    copies = [
-        pltpu.make_async_copy(
+        return i + 1
+
+    copies = []
+    at = jnp.int32(0)
+    for k in range(pieces):
+        at = lax.while_loop(functools.partial(more, (k + 1) * size), step, at)
+        copy = pltpu.make_async_copy(
             table.at[pl.ds(k * size, size)], out_ref.at[pl.ds(k * size, size)], sems.at[k]
         )
-        for k in range(pieces)
-    ]
-    for copy in copies:
         copy.start()
+        copies.append(copy)
     store_b.wait()
     for copy in copies:
         copy.wait()
@@ -353,12 +417,15 @@
             pltpu.SMEM((1, members), jnp.int32),
             pltpu.VMEM((total // LANES, LANES), jnp.int32),
             pltpu.VMEM((total // LANES, LANES), jnp.float32),
+            pltpu.VMEM((total // LANES, LANES), jnp.float32),
+            pltpu.VMEM((total // LANES, LANES), jnp.float32),
+            pltpu.VMEM((total, 2 * LANES), jnp.bfloat16),
             pltpu.VMEM((ROWS, min(WIDE, total)), jnp.bfloat16),
             pltpu.VMEM((total, lanes), jnp.float32),
             pltpu.VMEM((members, cap, lanes), jnp.bfloat16),
             dma((members,)), dma((members,)), dma((members,)), dma((members,)),
             dma((members, groups)), dma((members, groups)), dma((groups,)), dma((groups,)),
-            dma((members,)), dma((members,)), dma((3,)), dma((groups,)),
+            dma((members,)), dma((members,)), dma((3,)), dma((total // ROWS,)),
         ],
         compiler_params=pltpu.CompilerParams(collective_id=0, has_side_effects=True),
     )(values, slots, counts)

time: 24.9 us -> 23.3 us (0.936)
  Pallas kernels: 24.1 us -> 22.3 us
    pallas_call x1, Pallas kernels: 5.41 us -> 3.73 us  [per_device(): pl.pallas_call(functools.partial(place_kernel, total), out_shape=(jax.Sha...]
where the time goes in v4:
time: 23.3 us; the launch traced here: 22.9 us
  Pallas kernels  22.3 us (96%)
  between operations  0.64 us (3%)
    pallas_call x1, Pallas kernels, per_device(): pl.pallas_call(functools.partial(exchange_kernel, groups, members, cap),...  18.6 us
    pallas_call x1, Pallas kernels, per_device(): pl.pallas_call(functools.partial(place_kernel, total), out_shape=(jax.Sha...  3.73 us

profile of v4, /device:TPU:0, one launch (start us, length us, event | category | flops | bytes accessed | tf_op | source)
XLA Modules:
  0.0 22.9 jit_solution(17271795484214042715)
XLA Ops:
  0.6 18.6 %shard_map.50 = (f32[1024,128]{1,0:T(8,128)}, s32[8,128]{1,0:T(8,128)}, bf16[8,32,128]{2,1,0:T(8,128)(2,1)}) custom-call(bf16[1,8,32,128]{3,2,1,0:T(8,128)(2,1)} %values_ref.1, s32[1,8,32]{2,1,0:T(8,128)} %slots_ref.1, s32[1,8]{1,0:T(1,128)} %counts_ref.1), custom_call_target="tpu_custom_call" | custom-call | tf_op jit(solution)/shard_map/pallas_call | solution.py:402
  19.2 3.7 %shard_map.51 = (f32[7168,128]{1,0:T(8,128)}, bf16[8,32,128]{2,1,0:T(8,128)(2,1)}) custom-call(f32[1024,128]{1,0:T(8,128)} %get-tuple-element.7.avg_ref, s32[8,128]{1,0:T(8,128)} %get-tuple-element.8.slot_ref, bf16[8,32,128]{2,1,0:T(8,128)(2,1)} %get-tuple-element.9.back_ref), custom_call_target="tpu_custom_call" | custom-call | tf_op jit(solution)/shard_map/pallas_call | solution.py:432

commit v5 on v4

--- a/solution.py
+++ b/solution.py
@@ -11,6 +11,7 @@
 LANES = 128
 ROWS = 256
 WIDE = 1024
+JOINED = 2
 
 
 def partner(index, step, count):
@@ -46,6 +47,7 @@
     m = lax.axis_index("mem")
     total = groups * members * cap
     per_row = LANES // cap
+    joined = 1 if members & (members - 1) else min(members, JOINED)
 
     def each(low, high, body):
         if high - low <= 8:
@@ -114,7 +116,7 @@
         )
 
     def to_group(step, hop):
-        at = g * members + origin(m, step, members)
+        at = pl.ds(g * members + origin(m - lax.rem(m, joined), step, members), joined)
         return pltpu.make_async_remote_copy(
             got.at[at], got.at[at], f_send.at[step, hop], f_recv.at[step, hop],
             device_id={"grp": target(g, hop, groups)},
@@ -122,7 +124,7 @@
 
     def from_group(step, hop):
         peer = origin(g, hop, groups)
-        at = peer * members + origin(m, step, members)
+        at = pl.ds(peer * members + origin(m - lax.rem(m, joined), step, members), joined)
         return pltpu.make_async_remote_copy(
             got.at[at], got.at[at], f_send.at[step, hop], f_recv.at[step, hop],
             device_id={"grp": peer},
@@ -147,8 +149,9 @@
     local_s = pltpu.make_async_copy(own_slots.at[m], got_slots.at[mine], local_sem.at[2])
     local_v.start()
     local_s.start()
-    each(1, members, lambda step: slots_to(step).start())
-    each(1, members, lambda step: to_member(step).start())
+    each(1, members, lambda step: slots_to(members - step).start())
+    to_member(1).start()
+    each(1, members - 1, lambda step: to_member(members - step).start())
     local_v.wait()
     local_s.wait()
 
@@ -156,18 +159,21 @@
         for hop in range(1, groups):
             to_group(step, hop).start()
 
+    each(1, joined, lambda step: from_member(step).wait_recv())
     forward(0)
 
-    def pass_on(step):
-        from_member(step).wait_recv()
-        forward(step)
-
-    early = members - members // 4
+    def pass_on(turn):
+        for k in range(joined):
+            from_member(turn * joined + k).wait_recv()
+        forward(turn * joined)
+
+    turns = members // joined
+    early = max(1, turns - max(1, turns // 4))
     each(1, early, pass_on)
     each(1, members, lambda step: slots_from(step).wait_recv())
     for hop in range(1, groups):
         slots_to_group(hop).start()
-    each(early, members, pass_on)
+    each(early, turns, pass_on)
     for hop in range(1, groups):
         slots_from_group(hop).wait_recv()
 
@@ -235,9 +241,9 @@
 
     def land(step):
         for hop in range(1, groups):
-            from_group(step, hop).wait_recv()
-
-    each(0, members, land)
+            from_group(step * joined, hop).wait_recv()
+
+    each(0, turns, land)
 
     def own_block(t):
         b = g * blocks_each + t
@@ -335,9 +341,9 @@
 
     def finish_forward(step):
         for hop in range(1, groups):
-            to_group(step, hop).wait_send()
-
-    each(0, members, finish_forward)
+            to_group(step * joined, hop).wait_send()
+
+    each(0, turns, finish_forward)
     each(1, members, lambda step: (to_member(step).wait_send(), slots_to(step).wait_send())[0])
     for hop in range(1, groups):
         slots_to_group(hop).wait_send()
@@ -349,7 +355,7 @@
 
 
 def place_kernel(total, avg_ref, slot_ref, back_ref, out_ref, returned_ref, table, rows, slot_s, back_v, in_sem, sems):
-    unroll = 32
+    unroll = LANES
     load_s = pltpu.make_async_copy(slot_ref, slot_s, in_sem.at[0])
     load_a = pltpu.make_async_copy(avg_ref, rows, in_sem.at[1])
     load_b = pltpu.make_async_copy(back_ref, back_v, in_sem.at[2])
@@ -368,15 +374,12 @@
     size = BUCKET // pieces
 
     def more(bound, i):
-        at = jnp.minimum(i, chunks - 1) * unroll
-        return jnp.logical_and(i < chunks, slot_s[at // LANES, lax.rem(at, LANES)] < bound)
+        return jnp.logical_and(i < chunks, slot_s[jnp.minimum(i, chunks - 1), 0] < bound)
 
     def step(i):
         base = pl.multiple_of(i * unroll, unroll)
-        row = base // LANES
-        col = lax.rem(base, LANES)
         for k in range(unroll):
-            s = slot_s[row, col + k]
+            s = slot_s[i, k]
             table[pl.ds(s, 1), :] = rows[pl.ds(base + k, 1), :]
         return i + 1
 

time: 23.3 us -> 22.3 us (0.957)
  Pallas kernels: 22.3 us -> 21.4 us
    pallas_call x1, Pallas kernels: 3.73 us -> 3.08 us  [per_device(): pl.pallas_call(functools.partial(place_kernel, total), out_shape=(jax.Sha...]
where the time goes in v5:
time: 22.3 us; the launch traced here: 22.1 us
  Pallas kernels  21.4 us (96%)
  between operations  0.64 us (3%)
    pallas_call x1, Pallas kernels, per_device(): pl.pallas_call(functools.partial(exchange_kernel, groups, members, cap),...  18.4 us
    pallas_call x1, Pallas kernels, per_device(): pl.pallas_call(functools.partial(place_kernel, total), out_shape=(jax.Sha...  3.08 us

profile of v5, /device:TPU:0, one launch (start us, length us, event | category | flops | bytes accessed | tf_op | source)
XLA Modules:
  0.0 22.1 jit_solution(11175915149598813724)
XLA Ops:
  0.6 18.4 %shard_map.50 = (f32[1024,128]{1,0:T(8,128)}, s32[8,128]{1,0:T(8,128)}, bf16[8,32,128]{2,1,0:T(8,128)(2,1)}) custom-call(bf16[1,8,32,128]{3,2,1,0:T(8,128)(2,1)} %values_ref.1, s32[1,8,32]{2,1,0:T(8,128)} %slots_ref.1, s32[1,8]{1,0:T(1,128)} %counts_ref.1), custom_call_target="tpu_custom_call" | custom-call | tf_op jit(solution)/shard_map/pallas_call | solution.py:405
  19.0 3.1 %shard_map.51 = (f32[7168,128]{1,0:T(8,128)}, bf16[8,32,128]{2,1,0:T(8,128)(2,1)}) custom-call(f32[1024,128]{1,0:T(8,128)} %get-tuple-element.7.avg_ref, s32[8,128]{1,0:T(8,128)} %get-tuple-element.8.slot_ref, bf16[8,32,128]{2,1,0:T(8,128)(2,1)} %get-tuple-element.9.back_ref), custom_call_target="tpu_custom_call" | custom-call | tf_op jit(solution)/shard_map/pallas_call | solution.py:435

commit v6 on v5

--- a/solution.py
+++ b/solution.py
@@ -268,7 +268,13 @@
             device_id={"mem": src},
         )
 
-    each(1, members, lambda step: back_to(members - step).start())
+    chips = members // 2
+    if chips == 4:
+        outer = jnp.where(lax.rem(m // 2 + 1, chips) < 2, 1, 0)
+        for lo, hi in ((6, 4), (7, 5), (4, 6), (5, 7), (2, 2), (3, 3), (1, 1)):
+            back_to(outer * lo + (1 - outer) * hi).start()
+    else:
+        each(1, members, lambda step: back_to(members - step).start())
     local_r = pltpu.make_async_copy(ret.at[m], back_ref.at[m], local_sem.at[2])
     local_r.start()
 
@@ -366,8 +372,6 @@
     table[...] = jnp.zeros_like(table)
     load_s.wait()
     load_a.wait()
-    load_b.wait()
-    store_b.start()
 
     chunks = total // unroll
     pieces = sems.shape[0]
@@ -392,6 +396,9 @@
         )
         copy.start()
         copies.append(copy)
+        if k == 0:
+            load_b.wait()
+            store_b.start()
     store_b.wait()
     for copy in copies:
         copy.wait()

time: 22.3 us -> 22.2 us (level)
  no operation moved by 1% of the time
where the time goes in v6:
time: 22.2 us; the launch traced here: 22 us
  Pallas kernels  21.4 us (96%)
  between operations  0.64 us (3%)
    pallas_call x1, Pallas kernels, per_device(): pl.pallas_call(functools.partial(exchange_kernel, groups, members, cap),...  18.3 us
    pallas_call x1, Pallas kernels, per_device(): pl.pallas_call(functools.partial(place_kernel, total), out_shape=(jax.Sha...  3.1 us

profile of v6, /device:TPU:0, one launch (start us, length us, event | category | flops | bytes accessed | tf_op | source)
XLA Modules:
  0.0 22.0 jit_solution(14116949947812564718)
XLA Ops:
  0.6 18.3 %shard_map.50 = (f32[1024,128]{1,0:T(8,128)}, s32[8,128]{1,0:T(8,128)}, bf16[8,32,128]{2,1,0:T(8,128)(2,1)}) custom-call(bf16[1,8,32,128]{3,2,1,0:T(8,128)(2,1)} %values_ref.1, s32[1,8,32]{2,1,0:T(8,128)} %slots_ref.1, s32[1,8]{1,0:T(1,128)} %counts_ref.1), custom_call_target="tpu_custom_call" | custom-call | tf_op jit(solution)/shard_map/pallas_call | solution.py:412
  18.9 3.1 %shard_map.51 = (f32[7168,128]{1,0:T(8,128)}, bf16[8,32,128]{2,1,0:T(8,128)(2,1)}) custom-call(f32[1024,128]{1,0:T(8,128)} %get-tuple-element.7.avg_ref, s32[8,128]{1,0:T(8,128)} %get-tuple-element.8.slot_ref, bf16[8,32,128]{2,1,0:T(8,128)(2,1)} %get-tuple-element.9.back_ref), custom_call_target="tpu_custom_call" | custom-call | tf_op jit(solution)/shard_map/pallas_call | solution.py:442
